TPU v7x, 32 devices: a whole 2x2x4 slice. The times are simulated.
32 devices in a mesh: blk: 4 (over x, core), uly: 8 (over z, y).
Axes of the slice: x: 2, y: 2, z: 4, core: 2. Of those that a mesh axis runs over, the one named last changes fastest.
Arguments:
- query: bfloat16 [4096, 4096], P(('blk', 'uly')), may hold values from -5 to 5
- key_input: bfloat16 [4096, 512], P(('blk', 'uly')), may hold values from -5 to 5
- value_input: bfloat16 [4096, 512], P(('blk', 'uly')), may hold values from -6 to 6
- output: bfloat16 [4096, 4096], P(('blk', 'uly')), may hold values from -6 to 6
- out_grad: bfloat16 [4096, 4096], P(('blk', 'uly')), may hold values from -6 to 6
Outputs:
- query_grad: bfloat16 [4096, 4096], P(('blk', 'uly'))
- key_gradient: bfloat16 [4096, 512], P(('blk', 'uly'))
- value_gradient: bfloat16 [4096, 512], P(('blk', 'uly'))
All inputs are finite; a program needn't handle non-finite values.
Results may differ from a plain program's by a relative error of at most 0.009.
Values may be sent and summed in bfloat16 or wider, within the bound.
A program may use at most 64 MiB of HBM per device.

v0:
```python
import functools
import math

import jax
import jax.numpy as jnp
from jax import lax
from jax.experimental import pallas as pl
from jax.experimental.pallas import tpu as pltpu
from jax.sharding import PartitionSpec as P

QUERY_HEADS = 32
KEY_VALUE_HEADS = 4
HEAD_SIZE = 128
WINDOW_KEYS = 1024
GROUP = QUERY_HEADS // KEY_VALUE_HEADS
PAIRS = GROUP // 2
MESH = pl.DeviceIdType.MESH
F32 = jnp.float32
BF16 = jnp.bfloat16
NT = (((1,), (1,)), ((), ()))
TN = (((0,), (0,)), ((), ()))


def kernel(
    rows, back, blks, ulys,
    q_hbm, k_hbm, v_hbm, o_hbm, g_hbm,
    dq_ref, dk_ref, dv_ref,
    q_ref, o_ref, g_ref, kv, acc_k, acc_v, own, pg_send, pg_recv, c_send, c_recv,
    load_sem, kv_sem, chain_ss, chain_rs, pair_ss, pair_rs, pgs, pgr, cgs, cgr,
):
    half = back // 2
    heads = KEY_VALUE_HEADS
    scaling = HEAD_SIZE ** (-0.5)
    total = blks * ulys
    me = lax.axis_index("blk") * ulys + lax.axis_index("uly")
    par = lax.rem(me, 2)
    partner = me + 1 - 2 * par
    up, down = me + 2, me - 2
    has_up, has_down = up < total, down >= 0

    def where_is(t):
        return (t // ulys, lax.rem(t, ulys))

    loads = [
        pltpu.make_async_copy(s, d, load_sem.at[i])
        for i, (s, d) in enumerate(((q_hbm, q_ref), (o_hbm, o_ref), (g_hbm, g_ref)))
    ]
    kv_loads = []
    for h in range(heads):
        for i, src in enumerate((k_hbm, v_hbm)):
            kv_loads.append(
                pltpu.make_async_copy(
                    src.at[:, h * HEAD_SIZE : (h + 1) * HEAD_SIZE], kv.at[h, back, i], kv_sem.at[h, i]
                )
            )
    for copy in kv_loads:
        copy.start()
    for copy in loads:
        copy.start()

    barrier = pltpu.get_barrier_semaphore()

    @pl.when(has_up)
    def _():
        pl.semaphore_signal(barrier, inc=1, device_id=where_is(up), device_id_type=MESH)

    @pl.when(has_down)
    def _():
        pl.semaphore_signal(barrier, inc=1, device_id=where_is(down), device_id_type=MESH)

    pl.semaphore_signal(barrier, inc=1, device_id=where_is(partner), device_id_type=MESH)
    pl.semaphore_wait(barrier, 1 + has_up.astype(jnp.int32) + has_down.astype(jnp.int32))

    def clear(s, carry):
        @pl.when(me - back + s < 0)
        def _():
            for h in range(heads):
                kv[h, s] = jnp.zeros((2, rows, HEAD_SIZE), BF16)

        return carry

    lax.fori_loop(0, back, clear, 0)

    def chain_copy(h, k):
        return pltpu.make_async_remote_copy(
            src_ref=kv.at[h, back - 2 * k],
            dst_ref=kv.at[h, back - 2 * k - 2],
            send_sem=chain_ss.at[h, k],
            recv_sem=chain_rs.at[h, k],
            device_id=where_is(up),
            device_id_type=MESH,
        )

    def pair_copy(h, k):
        return pltpu.make_async_remote_copy(
            src_ref=kv.at[h, back - 2 * k - 2 * par],
            dst_ref=kv.at[h, back - 1 - 2 * k],
            send_sem=pair_ss.at[h, k],
            recv_sem=pair_rs.at[h, k],
            device_id=where_is(partner),
            device_id_type=MESH,
        )

    def chain_out(k):
        return has_up & (me - 2 * k >= 0)

    def pair_out(k):
        return me - 2 * k - 2 * par >= 0

    def send_own(h):
        @pl.when(has_up)
        def _():
            chain_copy(h, 0).start()

        @pl.when(par == 0)
        def _():
            pair_copy(h, 0).start()

    def gather_step(h, k):
        @pl.when(me - 2 * k - 2 >= 0)
        def _():
            chain_copy(h, k).wait_recv()

            @pl.when(has_up & (k < half - 1))
            def _():
                chain_copy(h, k + 1).start()

            nxt = k + 1 - par

            @pl.when(nxt < half)
            def _():
                pair_copy(h, nxt).start()

    def gather_finish(h, k):
        @pl.when(me - 1 - 2 * k >= 0)
        def _():
            pair_copy(h, k).wait_recv()

    def pg_copy(h, k):
        return pltpu.make_async_remote_copy(
            src_ref=pg_send.at[h, k],
            dst_ref=pg_recv.at[h, k],
            send_sem=pgs.at[h, k],
            recv_sem=pgr.at[h, k],
            device_id=where_is(partner),
            device_id_type=MESH,
        )

    def cg_copy(h, j):
        return pltpu.make_async_remote_copy(
            src_ref=c_send.at[h, j],
            dst_ref=c_recv.at[h, j],
            send_sem=cgs.at[h, j],
            recv_sem=cgr.at[h, j],
            device_id=where_is(down),
            device_id_type=MESH,
        )

    def pg_out(h, k):
        s = back - 1 - 2 * k
        at = pl.ds(s * rows, rows)
        pg_send[h, k, 0] = (acc_k[at, :] * scaling).astype(BF16)
        pg_send[h, k, 1] = acc_v[at, :].astype(BF16)

        @pl.when(me - 1 - 2 * k >= 0)
        def _():
            pg_copy(h, k).start()

    def keep_own(h, e):
        at = pl.ds((back - 2 * e) * rows, rows)
        own[h, e, 0] = acc_k[at, :] * scaling
        own[h, e, 1] = acc_v[at, :]

    def reduce_step(h, j):
        e = half - j

        @pl.when(me - 2 * e >= 0)
        def _():
            k = e - par

            @pl.when((k >= 0) & (k < half))
            def _():
                pg_copy(h, k).wait_recv()
                own[h, e] = own[h, e] + pg_recv[h, k].astype(F32)

            @pl.when(has_up & (j > 0))
            def _():
                cg_copy(h, j - 1).wait_recv()
                own[h, e] = own[h, e] + c_recv[h, j - 1].astype(F32)

    def reduce_send(h, j):
        @pl.when(me - 2 * (half - j) >= 0)
        def _():
            c_send[h, j] = own[h, half - j].astype(BF16)
            cg_copy(h, j).start()

    def finish(h):
        reduce_step(h, half)
        columns = pl.ds(pl.multiple_of(h * HEAD_SIZE, HEAD_SIZE), HEAD_SIZE)
        dk_ref[:, columns] = own[h, 0, 0].astype(BF16)
        dv_ref[:, columns] = own[h, 0, 1].astype(BF16)

    def compute(h, p):
        first = pl.multiple_of((h * GROUP + 2 * p) * HEAD_SIZE, HEAD_SIZE)
        second = pl.multiple_of(first + HEAD_SIZE, HEAD_SIZE)

        def two(ref):
            return jnp.concatenate(
                [ref[:, pl.ds(first, HEAD_SIZE)], ref[:, pl.ds(second, HEAD_SIZE)]], axis=0
            )

        q2, g2, o2 = two(q_ref), two(g_ref), two(o_ref)
        rd = jnp.sum((o2.astype(F32) * g2.astype(F32)).T, axis=0, keepdims=True)
        keys = kv[h, :, 0].reshape((back + 1) * rows, HEAD_SIZE)
        values = kv[h, :, 1].reshape((back + 1) * rows, HEAD_SIZE)
        st = lax.dot_general(keys, q2, NT, preferred_element_type=F32)
        dp = lax.dot_general(values, g2, NT, preferred_element_type=F32)
        key_at = lax.broadcasted_iota(jnp.int32, (rows, 2 * rows), 0)
        query_at = lax.rem(lax.broadcasted_iota(jnp.int32, (rows, 2 * rows), 1), rows)
        tri = key_at > query_at
        gone = [jnp.where(me - back + s < 0, 1e30, 0.0).astype(F32) for s in range(back)]

        def cut(a, s):
            return a[s * rows : (s + 1) * rows]

        c = scaling * math.log2(math.e)
        blocks = [jnp.where(tri, cut(st, 0) - gone[0], cut(st, back))]
        blocks += [cut(st, s) for s in range(1, back)]
        top = jnp.max(blocks[0], axis=0, keepdims=True)
        for s in range(1, back):
            top = jnp.maximum(top, jnp.max(blocks[s], axis=0, keepdims=True) - gone[s])
        top = top * c
        probs = [jnp.exp2(blocks[0] * c - top)]
        probs += [jnp.exp2(blocks[s] * c - (top + gone[s])) for s in range(1, back)]
        sums = jnp.sum(probs[0], axis=0, keepdims=True)
        for s in range(1, back):
            sums = sums + jnp.sum(probs[s], axis=0, keepdims=True)
        inv = 1.0 / sums
        dps = [jnp.where(tri, cut(dp, 0), cut(dp, back))] + [cut(dp, s) for s in range(1, back)]
        ws = [a * inv for a in probs]
        ds = [w * (a - rd) for w, a in zip(ws, dps)]

        def spread(parts):
            low = [jnp.where(tri, parts[0], 0.0)] + parts[1:] + [jnp.where(tri, 0.0, parts[0])]
            return jnp.concatenate([a.astype(BF16) for a in low], axis=0)

        wt, dst = spread(ws), spread(ds)
        acc_v[...] += jnp.dot(wt, g2, preferred_element_type=F32)
        acc_k[...] += jnp.dot(dst, q2, preferred_element_type=F32)
        dq = lax.dot_general(dst, keys, TN, preferred_element_type=F32) * scaling
        dq_ref[:, pl.ds(first, HEAD_SIZE)] = dq[:rows].astype(BF16)
        dq_ref[:, pl.ds(second, HEAD_SIZE)] = dq[rows:].astype(BF16)

    for h in range(heads):
        kv_loads[2 * h].wait()
        kv_loads[2 * h + 1].wait()
        send_own(h)

    def loop(count, fn):
        def body(i, carry):
            fn(i)
            return carry

        lax.fori_loop(0, count, body, 0)

    def hop(k):
        loop(heads, lambda h: gather_step(h, k))

    loop(half - 1, hop)
    gather_step(0, half - 1)
    for copy in loads:
        copy.wait()

    def job(h, j):
        @pl.when((h >= 0) & (h < heads) & (j < half))
        def _():
            reduce_step(h, j)
            reduce_send(h, j)

        @pl.when((h >= 0) & (h < heads) & (j == half))
        def _():
            finish(h)

    lag = half + 1

    def per_head(h):
        @pl.when(h < heads)
        def _():
            loop(half, lambda k: gather_finish(h, k))
            acc_k[...] = jnp.zeros_like(acc_k)
            acc_v[...] = jnp.zeros_like(acc_v)

        def part(i):
            p = 2 * i

            @pl.when(h < heads)
            def _():
                compute(h, p)
                compute(h, p + 1)

            @pl.when((h == 0) & (p + 1 < heads))
            def _():
                gather_step(p + 1, half - 1)

            @pl.when((h == 0) & (p + 2 < heads))
            def _():
                gather_step(p + 2, half - 1)

        loop(PAIRS // 2, part)

        @pl.when(h < heads)
        def _():
            loop(half, lambda k: pg_out(h, k))
            loop(half + 1, lambda e: keep_own(h, e))

        for m in range(1, lag + 1):
            job(h - m, m - 1)

    loop(heads + lag, per_head)

    def drain(h):
        def inner(k):
            @pl.when(chain_out(k))
            def _():
                chain_copy(h, k).wait_send()

            @pl.when(pair_out(k))
            def _():
                pair_copy(h, k).wait_send()

            @pl.when(me - 1 - 2 * k >= 0)
            def _():
                pg_copy(h, k).wait_send()

            @pl.when(me - 2 * (half - k) >= 0)
            def _():
                cg_copy(h, k).wait_send()

        loop(half, inner)

    loop(heads, drain)


def local(query, key_input, value_input, output, out_grad):
    rows, width = query.shape
    blks, ulys = lax.axis_size("blk"), lax.axis_size("uly")
    back = WINDOW_KEYS // rows
    half = back // 2
    heads = KEY_VALUE_HEADS
    span = (back + 1) * rows
    pair = (2, rows, HEAD_SIZE)
    dma = pltpu.SemaphoreType.DMA
    any_spec = pl.BlockSpec(memory_space=pl.ANY)
    vmem_spec = pl.BlockSpec(memory_space=pltpu.VMEM)
    return pl.pallas_call(
        functools.partial(kernel, rows, back, blks, ulys),
        out_shape=(
            jax.ShapeDtypeStruct(query.shape, BF16),
            jax.ShapeDtypeStruct(key_input.shape, BF16),
            jax.ShapeDtypeStruct(value_input.shape, BF16),
        ),
        in_specs=[any_spec] * 5,
        out_specs=(vmem_spec,) * 3,
        scratch_shapes=[
            pltpu.VMEM((rows, width), BF16),
            pltpu.VMEM((rows, width), BF16),
            pltpu.VMEM((rows, width), BF16),
            pltpu.VMEM((heads, back + 1) + pair, BF16),
            pltpu.VMEM((span, HEAD_SIZE), F32),
            pltpu.VMEM((span, HEAD_SIZE), F32),
            pltpu.VMEM((heads, half + 1) + pair, F32),
            pltpu.VMEM((heads, half) + pair, BF16),
            pltpu.VMEM((heads, half) + pair, BF16),
            pltpu.VMEM((heads, half) + pair, BF16),
            pltpu.VMEM((heads, half) + pair, BF16),
            dma((3,)),
            dma((heads, 2)),
        ]
        + [dma((heads, half))] * 8,
        compiler_params=pltpu.CompilerParams(
            collective_id=0, has_side_effects=True, vmem_limit_bytes=60 * 1024 * 1024
        ),
    )(query, key_input, value_input, output, out_grad)


def solution(mesh):
    spec = P(("blk", "uly"), None)
    return jax.shard_map(
        local, mesh=mesh, in_specs=(spec,) * 5, out_specs=(spec,) * 3, check_vma=False
    )
```

profile of v0, /device:TPU:29, one launch (start us, length us, event | category | flops | bytes accessed | tf_op | source)
XLA Modules:
  0.0 80.9 jit_solution(15494828834606426264)
XLA Ops:
  0.6 76.3 %shard_map.76 = (bf16[128,4096]{1,0:T(8,128)(2,1)}, bf16[128,512]{1,0:T(8,128)(2,1)}, bf16[128,512]{1,0:T(8,128)(2,1)}) custom-call(bf16[128,4096]{1,0:T(8,128)(2,1)} %q_hbm.1, bf16[128,512]{1,0:T(8,128)(2,1)} %k_hbm.1, bf16[128,512]{1,0:T(8,128)(2,1)} %v_hbm.1, bf16[128,4096]{1,0:T(8,128)(2,1)} %o_hbm.1, bf16[128,4096]{1,0:T(8,128)(2,1)} %g_hbm.1), custom_call_target="tpu_custom_call" | custom-call | tf_op jit(solution)/shard_map/pallas_call | solution.py:355
  77.0 0.0 copy-start.1
  77.0 2.3 %copy.11 = bf16[128,4096]{1,0:T(8,128)(2,1)} copy(bf16[128,4096]{1,0:T(8,128)(2,1)} %get-tuple-element.6) | data formatting | bytes 2097152
  79.3 0.0 copy-done.1
  79.3 0.0 copy-start
  79.3 0.7 copy.12
  80.0 0.3 copy-done
  80.3 0.7 copy.13
Async XLA Ops:
  77.0 2.3 %copy-start.1 = (bf16[128,512]{1,0:T(8,128)(2,1)S(1)}, bf16[128,512]{1,0:T(8,128)(2,1)}, u32[]{:S(2)}) copy-start(bf16[128,512]{1,0:T(8,128)(2,1)} %get-tuple-element.7) | copy-start | bytes 393220
  79.3 1.0 %copy-start = (bf16[128,512]{1,0:T(8,128)(2,1)S(1)}, bf16[128,512]{1,0:T(8,128)(2,1)}, u32[]{:S(2)}) copy-start(bf16[128,512]{1,0:T(8,128)(2,1)} %get-tuple-element.8) | copy-start | bytes 393220
where the time goes:
time: 81.1 us; the launch traced here: 80.9 us
  Pallas kernels  76.3 us (94%)
  local copies, waits for them, and re-layouts  3.93 us (5%)
    pallas_call x1, Pallas kernels, local(): pl.pallas_call(functools.partial(kernel, rows, back, blks, ulys), out_sha...  76.3 us
    unnamed x7, local copies, waits for them, and re-layouts  3.93 us

commit v1 on v0

v1 whole, which is shorter than its diff:
```python
import functools
import math

import jax
import jax.numpy as jnp
from jax import lax
from jax.experimental import pallas as pl
from jax.experimental.pallas import tpu as pltpu
from jax.sharding import PartitionSpec as P

QUERY_HEADS = 32
KEY_VALUE_HEADS = 4
HEAD_SIZE = 128
WINDOW_KEYS = 1024
GROUP = QUERY_HEADS // KEY_VALUE_HEADS
PAIRS = GROUP // 2
AHEAD = 6
HOME_LAG = 1
FINISH_LAG = 6
WIDTH = 2
WIDE_GATHER = 1
WIDE_REDUCE = 0
WIDE_HOPS = ((0, 1, 3, 5),)
WIDE_LAG = 0
WIDE_GAP = 1
DIRECT = 0
EARLY = 3
SECOND = 0
WIDE_FIRST = -1
MESH = pl.DeviceIdType.MESH
F32 = jnp.float32
BF16 = jnp.bfloat16
NT = (((1,), (1,)), ((), ()))
TN = (((0,), (0,)), ((), ()))


def kernel(
    rows, back, blks, ulys,
    q_hbm, k_hbm, v_hbm, o_hbm, g_hbm,
    dq_hbm, dk_ref, dv_ref,
    dq_ref, q_ref, o_ref, g_ref, kv, acc_k, acc_v, pair_send, pair_recv, home_send, home_recv,
    relay_recv, load_sem, kv_sem, far_ss, far_rs, near_ss, near_rs, gn_ss, gn_rs, gf_ss, gf_rs,
    on_ss, rl_rs, ws_send, ws_recv, wl_send, wl_recv,
    wp_ss, wp_rs, wc_ss, wc_rs, gw_ss, gw_rs, gl_ss, gl_rs,
):
    half = back // 2
    heads = KEY_VALUE_HEADS
    scaling = HEAD_SIZE ** (-0.5)
    total = blks * ulys
    me = lax.axis_index("blk") * ulys + lax.axis_index("uly")
    par = lax.rem(me, 2)
    partner = me + 1 - 2 * par
    level = lax.rem(me, back) // 2
    up, down = me + 2, me - 2

    def where_is(t):
        return (t // ulys, lax.rem(t, ulys))

    loads = [
        pltpu.make_async_copy(s, d, load_sem.at[i])
        for i, (s, d) in enumerate(((q_hbm, q_ref), (o_hbm, o_ref), (g_hbm, g_ref)))
    ]
    dq_out = [pltpu.make_async_copy(dq_ref, dq_hbm, load_sem.at[3])]
    kv_loads = []
    for h in range(heads):
        for i, src in enumerate((k_hbm, v_hbm)):
            kv_loads.append(
                pltpu.make_async_copy(
                    src.at[:, h * HEAD_SIZE : (h + 1) * HEAD_SIZE], kv.at[h, back + 1, i], kv_sem.at[h, i]
                )
            )
    for copy in kv_loads:
        copy.start()
    for copy in loads:
        copy.start()

    def loop(count, fn):
        def body(i, carry):
            fn(i)
            return carry

        lax.fori_loop(0, count, body, 0)

    barrier = pltpu.get_barrier_semaphore()

    def greet(k):
        for there, peer in ((me + 2 * k + 2 < total, me + 2 * k + 2), (me - 2 * k - 2 >= 0, me - 2 * k - 2)):

            @pl.when(there)
            def _():
                pl.semaphore_signal(barrier, inc=1, device_id=where_is(peer), device_id_type=MESH)

    loop(half, greet)
    pl.semaphore_signal(barrier, inc=1, device_id=where_is(partner), device_id_type=MESH)

    @pl.when(me < back)
    def _():
        def clear(s):
            @pl.when(me - back + s < 0)
            def _():
                for h in range(heads):
                    kv[h, s + 1] = jnp.zeros((2, rows, HEAD_SIZE), BF16)

        loop(back, clear)

    later, earlier = (total - 1 - me) // 2, me // 2
    pl.semaphore_wait(barrier, 1 + jnp.minimum(later, half) + jnp.minimum(earlier, half))

    def remote(src, dst, ss, rs, target):
        return pltpu.make_async_remote_copy(
            src_ref=src, dst_ref=dst, send_sem=ss, recv_sem=rs,
            device_id=where_is(target), device_id_type=MESH,
        )

    def far(h, k):
        return remote(
            kv.at[h, back + 1], kv.at[h, back + 1 - 2 * k], far_ss.at[h, k - 1], far_rs.at[h, k - 1], me + 2 * k
        )

    def near(h, k):
        return remote(
            kv.at[h, back + 1 - 2 * k - 2 * par], kv.at[h, back - 2 * k],
            near_ss.at[h, k], near_rs.at[h, k], partner,
        )

    rises = (level >= 2) & (level < half - 1)
    falls = (me >= back) & (level > 0) & (level + 2 < half)

    def far_out(k, h=None):
        away = jnp.where(level + k < half, k, half - k)
        straight = away != 3
        if h is not None:
            straight = straight | (h < DIRECT)
        return (me + 2 * k < total) & straight

    def onward(h, k, to, target):
        return remote(
            kv.at[h, back + 1 - 2 * k], kv.at[h, back + 1 - 2 * to], on_ss.at[h], far_rs.at[h, to - 1], target
        )

    def turn(q):
        top = jnp.where(q < 2, half - 1 + q, half - q)
        inner = jnp.where(q < 2, half - q, q - 1)
        return jnp.where(level == half - 1, top, jnp.where(level == 0, q + 1, inner))

    def far_in(k):
        return me - 2 * k >= 0

    def near_out(k):
        return me - 2 * k - 2 * par >= 0

    def near_in(k):
        return me - 1 - 2 * k >= 0

    def send_own(h):
        def one(i):
            k = half - i

            @pl.when(far_out(k, h))
            def _():
                far(h, k).start()

        loop(half, one)

        @pl.when(par == 0)
        def _():
            near(h, 0).start()

    def hand_on(h, k):
        @pl.when(far_in(k))
        def _():
            far(h, k).wait_recv()

            @pl.when((k == 2) & rises & (h >= DIRECT))
            def _():
                onward(h, k, k + 1, up).start()

            @pl.when((k == half - 2) & falls & (h >= DIRECT))
            def _():
                onward(h, k, k - 1, down).start()

            @pl.when(k - par < half)
            def _():
                near(h, k - par).start()

    def gather_finish(h):
        def one(k):
            @pl.when(near_in(k))
            def _():
                near(h, k).wait_recv()

        loop(half, one)

    def gn(h, k):
        return remote(pair_send.at[h, k], pair_recv.at[h, k], gn_ss.at[h, k], gn_rs.at[h, k], partner)

    def gf(h, k):
        return remote(
            home_send.at[h, k - 1], home_recv.at[h, k - 1], gf_ss.at[h, k - 1], gf_rs.at[h, k - 1],
            me - 2 * k,
        )

    def reduce_pair(h, k):
        pair_send[h, k, 0] = (acc_k[h, back - 2 * k] * scaling).astype(BF16)
        pair_send[h, k, 1] = acc_v[h, back - 2 * k].astype(BF16)

        @pl.when(near_in(k))
        def _():
            gn(h, k).start()

    def relay(h, k, target):
        return remote(home_send.at[h, k - 1], relay_recv.at[h], gf_ss.at[h, k - 1], rl_rs.at[h], target)

    def reduce_home(h, k):
        n = k - par
        at = back + 1 - 2 * k
        rise = (k == 3) & (k <= level)
        fall = (k == half - 3) & (k > level)

        @pl.when(far_in(k))
        def _():
            @pl.when(n < half)
            def _():
                gn(h, n).wait_recv()

            @pl.when(((k == 2) & rises) | ((k == half - 2) & falls))
            def _():
                relay(h, k, up).wait_recv()
                acc_k[h, at] += relay_recv[h, 0].astype(F32) * (1.0 / scaling)
                acc_v[h, at] += relay_recv[h, 1].astype(F32)

            @pl.when(n < half)
            def _():
                home_send[h, k - 1, 0] = (acc_k[h, at] * scaling + pair_recv[h, n, 0].astype(F32)).astype(BF16)
                home_send[h, k - 1, 1] = (acc_v[h, at] + pair_recv[h, n, 1].astype(F32)).astype(BF16)

            @pl.when(n == half)
            def _():
                home_send[h, k - 1, 0] = (acc_k[h, at] * scaling).astype(BF16)
                home_send[h, k - 1, 1] = acc_v[h, at].astype(BF16)

            @pl.when(rise)
            def _():
                relay(h, k, down).start()

            @pl.when(fall)
            def _():
                relay(h, k, up).start()

            @pl.when(jnp.logical_not(rise | fall))
            def _():
                gf(h, k).start()

    def reduce_finish(h):
        acc_k[h, back + 1] = acc_k[h, back + 1] * scaling

        @pl.when(par == 0)
        def _():
            gn(h, 0).wait_recv()
            acc_k[h, back + 1] += pair_recv[h, 0, 0].astype(F32)
            acc_v[h, back + 1] += pair_recv[h, 0, 1].astype(F32)

        def one(i):
            k = i + 1

            @pl.when(far_out(k))
            def _():
                gf(h, k).wait_recv()
                acc_k[h, back + 1] += home_recv[h, i, 0].astype(F32)
                acc_v[h, back + 1] += home_recv[h, i, 1].astype(F32)

        loop(half, one)
        columns = pl.ds(pl.multiple_of(h * HEAD_SIZE, HEAD_SIZE), HEAD_SIZE)
        dk_ref[:, columns] = acc_k[h, back + 1].astype(BF16)
        dv_ref[:, columns] = acc_v[h, back + 1].astype(BF16)

    has_up, has_down = level < half - 1, level > 0
    after, before = me + back, me - back
    has_after, has_before = after < total, before >= 0

    def two_at(k):
        return pl.ds(back + 1 - 2 * k - par, 2)

    def wide_pair(h, w):
        return remote(
            kv.at[h, back + 1], kv.at[h, back + 2 * par], wp_ss.at[w], wp_rs.at[w], partner
        )

    def wide_chain(h, w, k, to, target, s):
        return remote(
            kv.at[h, two_at(k)], kv.at[h, two_at(to)], wc_ss.at[w, s], wc_rs.at[w, to], target
        )

    def wide_start(h, w):
        wide_pair(h, w).wait_recv()

        @pl.when(has_after)
        def _():
            wide_chain(h, w, 0, half, after, half + 1).start()

        @pl.when(has_up)
        def _():
            wide_chain(h, w, 0, 1, up, 0).start()

    def wide_hop(h, w, n):
        @pl.when(n <= level)
        def _():
            wide_chain(h, w, n - 1, n, down, 0).wait_recv()

            @pl.when(has_up)
            def _():
                wide_chain(h, w, n, n + 1, up, n).start()

        k = half + 1 - n

        @pl.when(has_before & (k > level))
        def _():
            wide_chain(h, w, 0, k, up, 0).wait_recv()

            @pl.when(has_down)
            def _():
                wide_chain(h, w, k, k - 1, down, k).start()

    def wide_sum(w, e, to, target):
        return remote(ws_send.at[w, e], ws_recv.at[w, to], gw_ss.at[w, e], gw_rs.at[w, to], target)

    def wide_last(w):
        return remote(wl_send.at[w], wl_recv.at[w], gl_ss.at[w], gl_rs.at[w], partner)

    def wide_step(h, w, j):
        @pl.when(j == 0)
        def _():
            acc_k[h] = acc_k[h] * scaling

        def take(slot, at):
            acc_k[h, at] += ws_recv[w, slot, 0].astype(F32)
            acc_v[h, at] += ws_recv[w, slot, 1].astype(F32)

        def pack(e):
            ws_send[w, e, 0] = acc_k[h, two_at(e)].astype(BF16)
            ws_send[w, e, 1] = acc_v[h, two_at(e)].astype(BF16)

        e = half - 1 - j

        @pl.when((e <= level) & (e >= 0))
        def _():
            @pl.when(has_up)
            def _():
                wide_sum(w, 0, e, up).wait_recv()
                take(e, two_at(e))

            @pl.when(e > 0)
            def _():
                pack(e)
                wide_sum(w, e, e - 1, down).start()

        f = j + 1

        @pl.when(has_before & (f > level) & (f <= half))
        def _():
            @pl.when(has_down)
            def _():
                wide_sum(w, 0, f, down).wait_recv()
                take(f, two_at(f))

            pack(f)

            @pl.when(f < half)
            def _():
                wide_sum(w, f, f + 1, up).start()

            @pl.when(f == half)
            def _():
                wide_sum(w, f, half + 1, before).start()

        @pl.when(j == half)
        def _():
            @pl.when(has_after)
            def _():
                wide_sum(w, 0, half + 1, after).wait_recv()
                take(half + 1, two_at(0))

            other = back + 2 - 2 * par
            wl_send[w, 0] = acc_k[h, other].astype(BF16)
            wl_send[w, 1] = acc_v[h, other].astype(BF16)
            wide_last(w).start()

        @pl.when(j == half + 1)
        def _():
            wide_last(w).wait_recv()
            columns = slice(h * HEAD_SIZE, (h + 1) * HEAD_SIZE)
            dk_ref[:, columns] = (acc_k[h, back + 1] + wl_recv[w, 0].astype(F32)).astype(BF16)
            dv_ref[:, columns] = (acc_v[h, back + 1] + wl_recv[w, 1].astype(F32)).astype(BF16)

    def compute(h, p):
        first = pl.multiple_of((h * GROUP + 2 * p) * HEAD_SIZE, HEAD_SIZE)
        second = pl.multiple_of(first + HEAD_SIZE, HEAD_SIZE)

        def two(ref):
            return jnp.concatenate(
                [ref[:, pl.ds(first, HEAD_SIZE)], ref[:, pl.ds(second, HEAD_SIZE)]], axis=0
            )

        q2, g2, o2 = two(q_ref), two(g_ref), two(o_ref)
        rd = jnp.sum((o2.astype(F32) * g2.astype(F32)).T, axis=0, keepdims=True)
        keys = kv[h, 1 : back + 2, 0].reshape((back + 1) * rows, HEAD_SIZE)
        values = kv[h, 1 : back + 2, 1].reshape((back + 1) * rows, HEAD_SIZE)
        st = lax.dot_general(keys, q2, NT, preferred_element_type=F32)
        dp = lax.dot_general(values, g2, NT, preferred_element_type=F32)
        key_at = lax.broadcasted_iota(jnp.int32, (rows, 2 * rows), 0)
        query_at = lax.rem(lax.broadcasted_iota(jnp.int32, (rows, 2 * rows), 1), rows)
        tri = key_at > query_at
        gone = [jnp.where(me - back + s < 0, 1e30, 0.0).astype(F32) for s in range(back)]

        def cut(a, s):
            return a[s * rows : (s + 1) * rows]

        c = scaling * math.log2(math.e)
        blocks = [jnp.where(tri, cut(st, 0) - gone[0], cut(st, back))]
        blocks += [cut(st, s) for s in range(1, back)]
        top = jnp.max(blocks[0], axis=0, keepdims=True)
        for s in range(1, back):
            top = jnp.maximum(top, jnp.max(blocks[s], axis=0, keepdims=True) - gone[s])
        top = top * c
        probs = [jnp.exp2(blocks[0] * c - top)]
        probs += [jnp.exp2(blocks[s] * c - (top + gone[s])) for s in range(1, back)]
        sums = jnp.sum(probs[0], axis=0, keepdims=True)
        for s in range(1, back):
            sums = sums + jnp.sum(probs[s], axis=0, keepdims=True)
        inv = 1.0 / sums
        dps = [jnp.where(tri, cut(dp, 0), cut(dp, back))] + [cut(dp, s) for s in range(1, back)]
        ws = [a * inv for a in probs]
        ds = [w * (a - rd) for w, a in zip(ws, dps)]

        def spread(parts):
            low = [jnp.where(tri, parts[0], 0.0)] + parts[1:] + [jnp.where(tri, 0.0, parts[0])]
            return jnp.concatenate([a.astype(BF16) for a in low], axis=0)

        wt, dst = spread(ws), spread(ds)
        shape = (back + 1, rows, HEAD_SIZE)
        acc_v[h, 1 : back + 2] += jnp.dot(wt, g2, preferred_element_type=F32).reshape(shape)
        acc_k[h, 1 : back + 2] += jnp.dot(dst, q2, preferred_element_type=F32).reshape(shape)
        dq = lax.dot_general(dst, keys, TN, preferred_element_type=F32) * scaling
        dq_ref[:, pl.ds(first, HEAD_SIZE)] = dq[:rows].astype(BF16)
        dq_ref[:, pl.ds(second, HEAD_SIZE)] = dq[rows:].astype(BF16)

    narrow = heads - WIDE_GATHER
    for h in range(heads):
        kv_loads[2 * h].wait()
        kv_loads[2 * h + 1].wait()

        if h < EARLY:
            send_own(h)
        elif h >= narrow:
            wide_pair(h, h - narrow).start()


    order = half - 1
    per = PAIRS // WIDTH
    count = heads * per
    each = half // per

    def hand_on_at(f):
        @pl.when(f < narrow * half)
        def _():
            hand_on(f // half, lax.rem(lax.rem(f, half) + order, half) + 1)

    acc_k[...] = jnp.zeros_like(acc_k)
    acc_v[...] = jnp.zeros_like(acc_v)
    loop(SECOND, hand_on_at)
    for h in range(EARLY, narrow):
        send_own(h)
    loop(half + AHEAD - SECOND, lambda f: hand_on_at(f + SECOND))
    if WIDE_FIRST < 0:
        for w in range(WIDE_GATHER):
            wide_start(narrow + w, w)
    for copy in loads:
        copy.wait()

    def drain_gather(h):
        @pl.when((rises | falls) & (h >= DIRECT))
        def _():
            onward(h, 0, 1, up).wait_send()

        def inner(i):
            @pl.when(far_out(i + 1, h))
            def _():
                far(h, i + 1).wait_send()

            @pl.when(near_out(i))
            def _():
                near(h, i).wait_send()

        loop(half, inner)

    def sent():
        loop(narrow, drain_gather)
        for w in range(WIDE_GATHER):
            h = narrow + w
            wide_pair(h, w).wait_send()

            @pl.when(has_up)
            def _():
                wide_chain(h, w, 0, 1, up, 0).wait_send()

            @pl.when(has_after)
            def _():
                wide_chain(h, w, 0, half, after, half + 1).wait_send()

            def inner(i):
                n = i + 1

                @pl.when((has_up & (n <= level)) | (has_down & has_before & (n > level)))
                def _():
                    wide_chain(h, w, n, n - 1, down, n).wait_send()

            loop(half, inner)

    def piece(c):
        h, i = c // per, lax.rem(c, per)

        @pl.when((c < narrow * per) & (i == 0))
        def _():
            gather_finish(h)

        @pl.when(c < count)
        def _():
            for n in range(WIDTH):
                compute(h, i * WIDTH + n)

        @pl.when((c >= WIDE_REDUCE * per) & (c < count) & (i == per - 1))
        def _():
            def one(q):
                n = turn(q) - 1 + par
                reduce_pair(h, jnp.where(n < half, n, 0))

            loop(half, one)

        loop(each, lambda n: hand_on_at(c * each + n + half + AHEAD))

        def home_at(n):
            late = (c - per) * each + n - HOME_LAG
            g = jnp.maximum(late, 0) // half

            @pl.when((late >= 0) & (g >= WIDE_REDUCE) & (g < heads))
            def _():
                reduce_home(g, turn(lax.rem(late, half)))

        loop(each, home_at)
        @pl.when(c == count)
        def _():
            sent()
            for copy in dq_out:
                copy.start()

        late = c - 2 * per - FINISH_LAG
        e = jnp.maximum(late, 0) // per

        @pl.when((late >= 0) & (e >= WIDE_REDUCE) & (e < heads) & (lax.rem(late, per) == 0))
        def _():
            reduce_finish(e)

        for w in range(WIDE_GATHER):
            if WIDE_FIRST >= 0:

                @pl.when(c == WIDE_FIRST)
                def _():
                    wide_start(narrow + w, w)

            for n, at in enumerate(WIDE_HOPS[w]):

                @pl.when(c == at)
                def _():
                    wide_hop(narrow + w, w, n + 1)

        for w in range(WIDE_REDUCE):
            step = c - (w + 1) * per + 1 - WIDE_LAG
            j = jnp.maximum(step, 0) // WIDE_GAP

            @pl.when((step >= 0) & (j < half + 2) & (j * WIDE_GAP == step))
            def _():
                wide_step(w, w, j)

    narrow_end = count + per + 1 + max(HOME_LAG, FINISH_LAG + per)
    wide_end = WIDE_REDUCE * per + WIDE_LAG + WIDE_GAP * (half + 1)
    loop(max(narrow_end, wide_end), piece)

    def drain_reduce(h):
        def inner(i):
            @pl.when(near_in(i))
            def _():
                gn(h, i).wait_send()

            @pl.when(far_in(i + 1))
            def _():
                gf(h, i + 1).wait_send()

        loop(half, inner)

    for copy in dq_out:
        copy.wait()
    loop(heads - WIDE_REDUCE, lambda i: drain_reduce(i + WIDE_REDUCE))
    for w in range(WIDE_REDUCE):
        wide_last(w).wait_send()

        def inner(i):
            n = i + 1

            @pl.when((n <= level) | has_before)
            def _():
                wide_sum(w, n, n - 1, down).wait_send()

        loop(half, inner)


def local(query, key_input, value_input, output, out_grad):
    rows, width = query.shape
    blks, ulys = lax.axis_size("blk"), lax.axis_size("uly")
    back = WINDOW_KEYS // rows
    half = back // 2
    heads = KEY_VALUE_HEADS
    one = (rows, HEAD_SIZE)
    pair = (2,) + one
    dma = pltpu.SemaphoreType.DMA
    vmem = pltpu.VMEM
    any_spec = pl.BlockSpec(memory_space=pl.ANY)
    vmem_spec = pl.BlockSpec(memory_space=vmem)
    return pl.pallas_call(
        functools.partial(kernel, rows, back, blks, ulys),
        out_shape=(
            jax.ShapeDtypeStruct(query.shape, BF16),
            jax.ShapeDtypeStruct(key_input.shape, BF16),
            jax.ShapeDtypeStruct(value_input.shape, BF16),
        ),
        in_specs=[any_spec] * 5,
        out_specs=(any_spec, vmem_spec, vmem_spec),
        scratch_shapes=[
            vmem((rows, width), BF16),
            vmem((rows, width), BF16),
            vmem((rows, width), BF16),
            vmem((rows, width), BF16),
            vmem((heads, back + 3) + pair, BF16),
            vmem((heads, back + 3) + one, F32),
            vmem((heads, back + 3) + one, F32),
            vmem((heads, half) + pair, BF16),
            vmem((heads, half) + pair, BF16),
            vmem((heads, half) + pair, BF16),
            vmem((heads, half) + pair, BF16),
            vmem((heads,) + pair, BF16),
            dma((4,)),
            dma((heads, 2)),
        ]
        + [dma((heads, half))] * 8
        + [dma((heads,))] * 2
        + [vmem((max(WIDE_REDUCE, 1), half + 2, 2, 2) + one, BF16)] * 2
        + [vmem((max(WIDE_REDUCE, 1), 2) + one, BF16)] * 2
        + [dma((max(WIDE_GATHER, 1),))] * 2
        + [dma((max(WIDE_GATHER, 1), half + 2))] * 2
        + [dma((max(WIDE_REDUCE, 1), half + 2))] * 2
        + [dma((max(WIDE_REDUCE, 1),))] * 2,
        compiler_params=pltpu.CompilerParams(
            collective_id=0, has_side_effects=True, vmem_limit_bytes=60 * 1024 * 1024
        ),
    )(query, key_input, value_input, output, out_grad)


def solution(mesh):
    spec = P(("blk", "uly"), None)
    return jax.shard_map(
        local, mesh=mesh, in_specs=(spec,) * 5, out_specs=(spec,) * 3, check_vma=False
    )
```

time: 81.1 us -> 66.6 us (0.82)
  the two profiles are of different devices: /device:TPU:29 before, /device:TPU:0 now
where the time goes in v1:
time: 66.6 us; the launch traced here: 66.4 us
  Pallas kernels  61.8 us (93%)
  local copies, waits for them, and re-layouts  3.93 us (6%)
    pallas_call x1, Pallas kernels, local(): pl.pallas_call(functools.partial(kernel, rows, back, blks, ulys), out_sha...  61.8 us
    unnamed x7, local copies, waits for them, and re-layouts  3.93 us

profile of v1, /device:TPU:0, one launch (start us, length us, event | category | flops | bytes accessed | tf_op | source)
XLA Modules:
  0.0 66.4 jit_solution(9605743004879223511)
XLA Ops:
  0.6 61.8 %shard_map.76 = (bf16[128,4096]{1,0:T(8,128)(2,1)}, bf16[128,512]{1,0:T(8,128)(2,1)}, bf16[128,512]{1,0:T(8,128)(2,1)}) custom-call(bf16[128,4096]{1,0:T(8,128)(2,1)} %q_hbm.1, bf16[128,512]{1,0:T(8,128)(2,1)} %k_hbm.1, bf16[128,512]{1,0:T(8,128)(2,1)} %v_hbm.1, bf16[128,4096]{1,0:T(8,128)(2,1)} %o_hbm.1, bf16[128,4096]{1,0:T(8,128)(2,1)} %g_hbm.1), custom_call_target="tpu_custom_call" | custom-call | tf_op jit(solution)/shard_map/pallas_call | solution.py:628
  62.5 0.0 copy-start.1
  62.5 2.3 %copy.11 = bf16[128,4096]{1,0:T(8,128)(2,1)} copy(bf16[128,4096]{1,0:T(8,128)(2,1)} %get-tuple-element.6) | data formatting | bytes 2097152
  64.8 0.0 copy-done.1
  64.8 0.0 copy-start
  64.8 0.7 copy.12
  65.5 0.3 copy-done
  65.8 0.7 copy.13
Async XLA Ops:
  62.5 2.3 %copy-start.1 = (bf16[128,512]{1,0:T(8,128)(2,1)S(1)}, bf16[128,512]{1,0:T(8,128)(2,1)}, u32[]{:S(2)}) copy-start(bf16[128,512]{1,0:T(8,128)(2,1)} %get-tuple-element.7) | copy-start | bytes 393220
  64.8 1.0 %copy-start = (bf16[128,512]{1,0:T(8,128)(2,1)S(1)}, bf16[128,512]{1,0:T(8,128)(2,1)}, u32[]{:S(2)}) copy-start(bf16[128,512]{1,0:T(8,128)(2,1)} %get-tuple-element.8) | copy-start | bytes 393220

commit v2 on v1

--- a/solution.py
+++ b/solution.py
@@ -14,19 +14,18 @@
 WINDOW_KEYS = 1024
 GROUP = QUERY_HEADS // KEY_VALUE_HEADS
 PAIRS = GROUP // 2
-AHEAD = 6
-HOME_LAG = 1
-FINISH_LAG = 6
+AHEAD = 4
+HOME_LAG = 2
+FINISH_LAG = 5
 WIDTH = 2
 WIDE_GATHER = 1
-WIDE_REDUCE = 0
-WIDE_HOPS = ((0, 1, 3, 5),)
-WIDE_LAG = 0
-WIDE_GAP = 1
+WIDE_REDUCE = 1
+WIDE_HOPS = ((-1,0,2,4,5),)
+WIDE_STEPS = ((2,4,9,10),)
+SEND_ORDER = lambda i, half: half - i
 DIRECT = 0
 EARLY = 3
 SECOND = 0
-WIDE_FIRST = -1
 MESH = pl.DeviceIdType.MESH
 F32 = jnp.float32
 BF16 = jnp.bfloat16
@@ -37,10 +36,10 @@
 def kernel(
     rows, back, blks, ulys,
     q_hbm, k_hbm, v_hbm, o_hbm, g_hbm,
-    dq_hbm, dk_ref, dv_ref,
-    dq_ref, q_ref, o_ref, g_ref, kv, acc_k, acc_v, pair_send, pair_recv, home_send, home_recv,
+    dq_hbm, dk_hbm, dv_hbm,
+    dq_ref, dk_ref, dv_ref, dots, q_ref, o_ref, g_ref, kv, acc_k, acc_v, pair_send, pair_recv, home_send, home_recv,
     relay_recv, load_sem, kv_sem, far_ss, far_rs, near_ss, near_rs, gn_ss, gn_rs, gf_ss, gf_rs,
-    on_ss, rl_rs, ws_send, ws_recv, wl_send, wl_recv,
+    on_ss, rl_rs, out_sem, ws_send, ws_recv, wl_send, wl_recv,
     wp_ss, wp_rs, wc_ss, wc_rs, gw_ss, gw_rs, gl_ss, gl_rs,
 ):
     half = back // 2
@@ -143,6 +142,11 @@
         inner = jnp.where(q < 2, half - q, q - 1)
         return jnp.where(level == half - 1, top, jnp.where(level == 0, q + 1, inner))
 
+    def arrival(q):
+        inner = jnp.where(q < 2, q, half + 1 - q)
+        there = jnp.where(level == half - 1, q, jnp.where(level == 0, half - q, inner))
+        return jnp.where(q == 0, half, there)
+
     def far_in(k):
         return me - 2 * k >= 0
 
@@ -154,7 +158,7 @@
 
     def send_own(h):
         def one(i):
-            k = half - i
+            k = SEND_ORDER(i, half)
 
             @pl.when(far_out(k, h))
             def _():
@@ -327,71 +331,85 @@
     def wide_last(w):
         return remote(wl_send.at[w], wl_recv.at[w], gl_ss.at[w], gl_rs.at[w], partner)
 
+    def wide_relay(w, k, target):
+        return remote(
+            ws_send.at[w, k], ws_recv.at[w, half + 1], gw_ss.at[w, k], gw_rs.at[w, half + 1], target
+        )
+
     def wide_step(h, w, j):
-        @pl.when(j == 0)
-        def _():
-            acc_k[h] = acc_k[h] * scaling
-
         def take(slot, at):
             acc_k[h, at] += ws_recv[w, slot, 0].astype(F32)
             acc_v[h, at] += ws_recv[w, slot, 1].astype(F32)
 
-        def pack(e):
-            ws_send[w, e, 0] = acc_k[h, two_at(e)].astype(BF16)
-            ws_send[w, e, 1] = acc_v[h, two_at(e)].astype(BF16)
-
-        e = half - 1 - j
-
-        @pl.when((e <= level) & (e >= 0))
-        def _():
-            @pl.when(has_up)
-            def _():
-                wide_sum(w, 0, e, up).wait_recv()
-                take(e, two_at(e))
-
-            @pl.when(e > 0)
-            def _():
-                pack(e)
-                wide_sum(w, e, e - 1, down).start()
-
-        f = j + 1
-
-        @pl.when(has_before & (f > level) & (f <= half))
-        def _():
-            @pl.when(has_down)
-            def _():
-                wide_sum(w, 0, f, down).wait_recv()
-                take(f, two_at(f))
-
-            pack(f)
-
-            @pl.when(f < half)
-            def _():
-                wide_sum(w, f, f + 1, up).start()
-
-            @pl.when(f == half)
-            def _():
-                wide_sum(w, f, half + 1, before).start()
-
-        @pl.when(j == half)
-        def _():
-            @pl.when(has_after)
-            def _():
-                wide_sum(w, 0, half + 1, after).wait_recv()
-                take(half + 1, two_at(0))
-
+        def send(k):
+            ws_send[w, k, 0] = acc_k[h, two_at(k)].astype(BF16)
+            ws_send[w, k, 1] = acc_v[h, two_at(k)].astype(BF16)
+            rise = (k == 3) & (k <= level)
+            fall = (k == half - 3) & (k > level)
+
+            @pl.when(rise)
+            def _():
+                wide_relay(w, k, down).start()
+
+            @pl.when(fall)
+            def _():
+                wide_relay(w, k, up).start()
+
+            @pl.when(jnp.logical_not(rise | fall))
+            def _():
+                wide_sum(w, k, k, me - 2 * k).start()
+
+        def joins(k):
+            return ((k == 2) & rises) | ((k == half - 2) & falls)
+
+        @pl.when(j == 0)
+        def _():
+            acc_k[h] = acc_k[h] * scaling
+
+            def one(q):
+                k = turn(q)
+
+                @pl.when(far_in(k) & jnp.logical_not(joins(k)))
+                def _():
+                    send(k)
+
+            loop(half, one)
+
+        @pl.when((j == 1) & (rises | falls))
+        def _():
+            k = jnp.where(rises, 2, half - 2)
+            wide_relay(w, 0, up).wait_recv()
+            take(half + 1, two_at(k))
+            send(k)
+
+        @pl.when(j == 2)
+        def _():
+            def one(i):
+                @pl.when(far_out(i + 1))
+                def _():
+                    wide_sum(w, 0, i + 1, up).wait_recv()
+                    take(i + 1, two_at(0))
+
+            loop(half, one)
             other = back + 2 - 2 * par
             wl_send[w, 0] = acc_k[h, other].astype(BF16)
             wl_send[w, 1] = acc_v[h, other].astype(BF16)
             wide_last(w).start()
 
-        @pl.when(j == half + 1)
+        @pl.when(j == 3)
         def _():
             wide_last(w).wait_recv()
             columns = slice(h * HEAD_SIZE, (h + 1) * HEAD_SIZE)
             dk_ref[:, columns] = (acc_k[h, back + 1] + wl_recv[w, 0].astype(F32)).astype(BF16)
             dv_ref[:, columns] = (acc_v[h, back + 1] + wl_recv[w, 1].astype(F32)).astype(BF16)
 
+    def dot_rows(n):
+        first = pl.multiple_of(2 * n * HEAD_SIZE, HEAD_SIZE)
+        for i in range(2):
+            at = pl.ds(pl.multiple_of(first + i * HEAD_SIZE, HEAD_SIZE), HEAD_SIZE)
+            product = o_ref[:, at].astype(F32) * g_ref[:, at].astype(F32)
+            dots[n, :, i * rows : (i + 1) * rows] = jnp.sum(product.T, axis=0, keepdims=True)
+
     def compute(h, p):
         first = pl.multiple_of((h * GROUP + 2 * p) * HEAD_SIZE, HEAD_SIZE)
         second = pl.multiple_of(first + HEAD_SIZE, HEAD_SIZE)
@@ -401,8 +419,8 @@
                 [ref[:, pl.ds(first, HEAD_SIZE)], ref[:, pl.ds(second, HEAD_SIZE)]], axis=0
             )
 
-        q2, g2, o2 = two(q_ref), two(g_ref), two(o_ref)
-        rd = jnp.sum((o2.astype(F32) * g2.astype(F32)).T, axis=0, keepdims=True)
+        q2, g2 = two(q_ref), two(g_ref)
+        rd = dots[h * PAIRS + p]
         keys = kv[h, 1 : back + 2, 0].reshape((back + 1) * rows, HEAD_SIZE)
         values = kv[h, 1 : back + 2, 1].reshape((back + 1) * rows, HEAD_SIZE)
         st = lax.dot_general(keys, q2, NT, preferred_element_type=F32)
@@ -455,7 +473,6 @@
             wide_pair(h, h - narrow).start()
 
 
-    order = half - 1
     per = PAIRS // WIDTH
     count = heads * per
     each = half // per
@@ -463,20 +480,30 @@
     def hand_on_at(f):
         @pl.when(f < narrow * half)
         def _():
-            hand_on(f // half, lax.rem(lax.rem(f, half) + order, half) + 1)
+            hand_on(f // half, arrival(lax.rem(f, half)))
 
     acc_k[...] = jnp.zeros_like(acc_k)
     acc_v[...] = jnp.zeros_like(acc_v)
+    for copy in loads:
+        copy.wait()
+    loop(heads * PAIRS, dot_rows)
     loop(SECOND, hand_on_at)
     for h in range(EARLY, narrow):
         send_own(h)
-    loop(half + AHEAD - SECOND, lambda f: hand_on_at(f + SECOND))
-    if WIDE_FIRST < 0:
-        for w in range(WIDE_GATHER):
+    reached = SECOND
+    events = sorted(
+        (at, w, n) for w in range(WIDE_GATHER) for n, at in enumerate(WIDE_HOPS[w]) if at < 0
+    )
+    for at, w, n in events:
+        upto = half + AHEAD + at + 1
+        if upto > reached:
+            loop(upto - reached, lambda f, first=reached: hand_on_at(f + first))
+            reached = upto
+        if n == 0:
             wide_start(narrow + w, w)
-    for copy in loads:
-        copy.wait()
-
+        else:
+            wide_hop(narrow + w, w, n)
+    loop(half + AHEAD - reached, lambda f: hand_on_at(f + reached))
     def drain_gather(h):
         @pl.when((rises | falls) & (h >= DIRECT))
         def _():
@@ -516,6 +543,25 @@
 
             loop(half, inner)
 
+    def results(h):
+        columns = pl.ds(pl.multiple_of(h * HEAD_SIZE, HEAD_SIZE), HEAD_SIZE)
+        return [
+            pltpu.make_async_copy(s.at[:, columns], d.at[:, columns], out_sem.at[i, h])
+            for i, (s, d) in enumerate(((dk_ref, dk_hbm), (dv_ref, dv_hbm)))
+        ]
+
+    def drain_reduce(h):
+        def inner(i):
+            @pl.when(near_in(i))
+            def _():
+                gn(h, i).wait_send()
+
+            @pl.when(far_in(i + 1))
+            def _():
+                gf(h, i + 1).wait_send()
+
+        loop(half, inner)
+
     def piece(c):
         h, i = c // per, lax.rem(c, per)
 
@@ -558,48 +604,47 @@
 
         @pl.when((late >= 0) & (e >= WIDE_REDUCE) & (e < heads) & (lax.rem(late, per) == 0))
         def _():
+            @pl.when(e == heads - 1)
+            def _():
+                loop(heads - 1 - WIDE_REDUCE, lambda i: drain_reduce(i + WIDE_REDUCE))
+
             reduce_finish(e)
+            for copy in results(e):
+                copy.start()
 
         for w in range(WIDE_GATHER):
-            if WIDE_FIRST >= 0:
-
-                @pl.when(c == WIDE_FIRST)
-                def _():
-                    wide_start(narrow + w, w)
-
             for n, at in enumerate(WIDE_HOPS[w]):
+                if at >= 0:
+
+                    @pl.when(c == at)
+                    def _():
+                        if n == 0:
+                            wide_start(narrow + w, w)
+                        else:
+                            wide_hop(narrow + w, w, n)
+
+        for w in range(WIDE_REDUCE):
+            for j, at in enumerate(WIDE_STEPS[w]):
 
                 @pl.when(c == at)
                 def _():
-                    wide_hop(narrow + w, w, n + 1)
-
-        for w in range(WIDE_REDUCE):
-            step = c - (w + 1) * per + 1 - WIDE_LAG
-            j = jnp.maximum(step, 0) // WIDE_GAP
-
-            @pl.when((step >= 0) & (j < half + 2) & (j * WIDE_GAP == step))
-            def _():
-                wide_step(w, w, j)
+                    wide_step(w, w, j)
+                    if j == 3:
+                        for copy in results(w):
+                            copy.start()
 
     narrow_end = count + per + 1 + max(HOME_LAG, FINISH_LAG + per)
-    wide_end = WIDE_REDUCE * per + WIDE_LAG + WIDE_GAP * (half + 1)
-    loop(max(narrow_end, wide_end), piece)
-
-    def drain_reduce(h):
-        def inner(i):
-            @pl.when(near_in(i))
-            def _():
-                gn(h, i).wait_send()
-
-            @pl.when(far_in(i + 1))
-            def _():
-                gf(h, i + 1).wait_send()
-
-        loop(half, inner)
+    loop(max(narrow_end, 1 + max(max(steps) for steps in WIDE_STEPS)), piece)
 
     for copy in dq_out:
         copy.wait()
-    loop(heads - WIDE_REDUCE, lambda i: drain_reduce(i + WIDE_REDUCE))
+
+    def done(h):
+        for copy in results(h):
+            copy.wait()
+
+    loop(heads, done)
+    drain_reduce(heads - 1)
     for w in range(WIDE_REDUCE):
         wide_last(w).wait_send()
 
@@ -624,7 +669,6 @@
     dma = pltpu.SemaphoreType.DMA
     vmem = pltpu.VMEM
     any_spec = pl.BlockSpec(memory_space=pl.ANY)
-    vmem_spec = pl.BlockSpec(memory_space=vmem)
     return pl.pallas_call(
         functools.partial(kernel, rows, back, blks, ulys),
         out_shape=(
@@ -633,9 +677,12 @@
             jax.ShapeDtypeStruct(value_input.shape, BF16),
         ),
         in_specs=[any_spec] * 5,
-        out_specs=(any_spec, vmem_spec, vmem_spec),
+        out_specs=(any_spec,) * 3,
         scratch_shapes=[
             vmem((rows, width), BF16),
+            vmem(key_input.shape, BF16),
+            vmem(value_input.shape, BF16),
+            vmem((heads * PAIRS, 1, 2 * rows), F32),
             vmem((rows, width), BF16),
             vmem((rows, width), BF16),
             vmem((rows, width), BF16),
@@ -652,6 +699,7 @@
         ]
         + [dma((heads, half))] * 8
         + [dma((heads,))] * 2
+        + [dma((2, heads))]
         + [vmem((max(WIDE_REDUCE, 1), half + 2, 2, 2) + one, BF16)] * 2
         + [vmem((max(WIDE_REDUCE, 1), 2) + one, BF16)] * 2
         + [dma((max(WIDE_GATHER, 1),))] * 2

time: 66.6 us -> 64.9 us (0.974)
  Pallas kernels: 61.8 us -> 60.1 us
    pallas_call x1, Pallas kernels: 61.8 us -> 60.1 us  [local(): pl.pallas_call(functools.partial(kernel, rows, back, blks, ulys), out_sha...]
where the time goes in v2:
time: 64.9 us; the launch traced here: 64.7 us
  Pallas kernels  60.1 us (93%)
  local copies, waits for them, and re-layouts  3.93 us (6%)
  between operations  0.65 us (1%)
    pallas_call x1, Pallas kernels, local(): pl.pallas_call(functools.partial(kernel, rows, back, blks, ulys), out_sha...  60.1 us
    unnamed x7, local copies, waits for them, and re-layouts  3.93 us

profile of v2, /device:TPU:0, one launch (start us, length us, event | category | flops | bytes accessed | tf_op | source)
XLA Modules:
  0.0 64.7 jit_solution(515616071577566399)
XLA Ops:
  0.6 60.1 %shard_map.76 = (bf16[128,4096]{1,0:T(8,128)(2,1)}, bf16[128,512]{1,0:T(8,128)(2,1)}, bf16[128,512]{1,0:T(8,128)(2,1)}) custom-call(bf16[128,4096]{1,0:T(8,128)(2,1)} %q_hbm.1, bf16[128,512]{1,0:T(8,128)(2,1)} %k_hbm.1, bf16[128,512]{1,0:T(8,128)(2,1)} %v_hbm.1, bf16[128,4096]{1,0:T(8,128)(2,1)} %o_hbm.1, bf16[128,4096]{1,0:T(8,128)(2,1)} %g_hbm.1), custom_call_target="tpu_custom_call" | custom-call | tf_op jit(solution)/shard_map/pallas_call | solution.py:672
  60.8 0.0 copy-start.1
  60.8 2.3 %copy.11 = bf16[128,4096]{1,0:T(8,128)(2,1)} copy(bf16[128,4096]{1,0:T(8,128)(2,1)} %get-tuple-element.6) | data formatting | bytes 2097152
  63.1 0.0 copy-done.1
  63.1 0.0 copy-start
  63.1 0.7 %copy.12 = bf16[128,512]{1,0:T(8,128)(2,1)} copy(bf16[128,512]{1,0:T(8,128)(2,1)S(1)} %copy-done.1) | data formatting | bytes 262144
  63.8 0.3 copy-done
  64.1 0.7 %copy.13 = bf16[128,512]{1,0:T(8,128)(2,1)} copy(bf16[128,512]{1,0:T(8,128)(2,1)S(1)} %copy-done) | data formatting | bytes 262144
Async XLA Ops:
  60.8 2.3 %copy-start.1 = (bf16[128,512]{1,0:T(8,128)(2,1)S(1)}, bf16[128,512]{1,0:T(8,128)(2,1)}, u32[]{:S(2)}) copy-start(bf16[128,512]{1,0:T(8,128)(2,1)} %get-tuple-element.7) | copy-start | bytes 393220
  63.1 1.0 %copy-start = (bf16[128,512]{1,0:T(8,128)(2,1)S(1)}, bf16[128,512]{1,0:T(8,128)(2,1)}, u32[]{:S(2)}) copy-start(bf16[128,512]{1,0:T(8,128)(2,1)} %get-tuple-element.8) | copy-start | bytes 393220

commit v3 on v2

--- a/solution.py
+++ b/solution.py
@@ -24,8 +24,8 @@
 WIDE_STEPS = ((2,4,9,10),)
 SEND_ORDER = lambda i, half: half - i
 DIRECT = 0
-EARLY = 3
-SECOND = 0
+EARLY = 2
+SECOND = 1
 MESH = pl.DeviceIdType.MESH
 F32 = jnp.float32
 BF16 = jnp.bfloat16

time: 64.9 us -> 64.9 us (level)
  no operation moved by 1% of the time
where the time goes in v3:
time: 64.9 us; the launch traced here: 64.7 us
  Pallas kernels  60.1 us (93%)
  local copies, waits for them, and re-layouts  3.93 us (6%)
  between operations  0.65 us (1%)
    pallas_call x1, Pallas kernels, local(): pl.pallas_call(functools.partial(kernel, rows, back, blks, ulys), out_sha...  60.1 us
    unnamed x7, local copies, waits for them, and re-layouts  3.93 us

profile of v3, /device:TPU:0, one launch (start us, length us, event | category | flops | bytes accessed | tf_op | source)
XLA Modules:
  0.0 64.7 jit_solution(7297530188241783217)
XLA Ops:
  0.6 60.1 %shard_map.76 = (bf16[128,4096]{1,0:T(8,128)(2,1)}, bf16[128,512]{1,0:T(8,128)(2,1)}, bf16[128,512]{1,0:T(8,128)(2,1)}) custom-call(bf16[128,4096]{1,0:T(8,128)(2,1)} %q_hbm.1, bf16[128,512]{1,0:T(8,128)(2,1)} %k_hbm.1, bf16[128,512]{1,0:T(8,128)(2,1)} %v_hbm.1, bf16[128,4096]{1,0:T(8,128)(2,1)} %o_hbm.1, bf16[128,4096]{1,0:T(8,128)(2,1)} %g_hbm.1), custom_call_target="tpu_custom_call" | custom-call | tf_op jit(solution)/shard_map/pallas_call | solution.py:672
  60.8 0.0 copy-start.1
  60.8 2.3 %copy.11 = bf16[128,4096]{1,0:T(8,128)(2,1)} copy(bf16[128,4096]{1,0:T(8,128)(2,1)} %get-tuple-element.6) | data formatting | bytes 2097152
  63.1 0.0 copy-done.1
  63.1 0.0 copy-start
  63.1 0.7 %copy.12 = bf16[128,512]{1,0:T(8,128)(2,1)} copy(bf16[128,512]{1,0:T(8,128)(2,1)S(1)} %copy-done.1) | data formatting | bytes 262144
  63.8 0.3 copy-done
  64.1 0.7 %copy.13 = bf16[128,512]{1,0:T(8,128)(2,1)} copy(bf16[128,512]{1,0:T(8,128)(2,1)S(1)} %copy-done) | data formatting | bytes 262144
Async XLA Ops:
  60.8 2.3 %copy-start.1 = (bf16[128,512]{1,0:T(8,128)(2,1)S(1)}, bf16[128,512]{1,0:T(8,128)(2,1)}, u32[]{:S(2)}) copy-start(bf16[128,512]{1,0:T(8,128)(2,1)} %get-tuple-element.7) | copy-start | bytes 393220
  63.1 1.0 %copy-start = (bf16[128,512]{1,0:T(8,128)(2,1)S(1)}, bf16[128,512]{1,0:T(8,128)(2,1)}, u32[]{:S(2)}) copy-start(bf16[128,512]{1,0:T(8,128)(2,1)} %get-tuple-element.8) | copy-start | bytes 393220
